TPU v7x, 256 devices: a whole 4x4x8 slice. The times are simulated.
256 devices in a mesh: space: 128 (over z, y, x), rep: 2 (over core).
Axes of the slice: x: 4, y: 4, z: 8, core: 2. Of those that a mesh axis runs over, the one named last changes fastest.
Arguments:
- halo_rows: bfloat16 [4, 16384, 256], P(None, 'space', 'rep'), may hold values from -6 to 6
- unmatched: int32 [4, 16384], P(None, 'space'), may hold values 0 or 1
- owner_id: int32 [4, 16384, 1], P(None, 'space'), may hold values from 0 to 127; in each aligned block of 128 rows (0 to 127, 128 to 255, ..., all dimensions but the last counted through in order) at most 2 rows name the same one
- cand_index: int32 [4, 16384, 16], P(None, 'space'), may hold values from 0 to 511
- lengths: int32 [4, 16384], P(None, 'space'), may hold values from 1 to 16
- choice_index: int32 [4, 16384], P(None, 'space'), may hold values from 0 to 15, as said below
- desc_rows: bfloat16 [4, 65536, 256], P(None, 'space', 'rep'), may hold values from -6 to 6
Outputs:
- phantom: bfloat16 [4, 16384, 256], P(None, 'space', 'rep')
- best_merit: bfloat16 [4, 16384], P(None, 'space')
Inputs may be any that keep to these rules, and one draw needn't show every extreme that they name: `owner_id`: in each aligned block of 128 halos (one region in one snapshot) no owner is named by more than 2 halos, a bound that some block reaches. `choice_index`: less than the halo's length.
All inputs are finite; a program needn't handle non-finite values. No bound on the sum of `unmatched` on one device may be relied on, other than what follows from the above.
Results may differ from a plain program's by a relative error of at most 0.001.
Values may be sent and summed in bfloat16 or wider, within the bound.
A program may use at most 64 MiB of HBM per device.

v0:
```python
import jax
import jax.numpy as jnp
from jax import lax
from jax.experimental import pallas as pl
from jax.experimental.pallas import tpu as pltpu
from jax.sharding import PartitionSpec as P

MESH = pl.DeviceIdType.MESH
PEERS = 128
HALOS = 128
CANDS = 512
SLOTS = 4
REQS = PEERS * SLOTS
HALF = 128
K = 16
ROWS = 16
NEG = -1e30
F32 = jnp.float32
BF16 = jnp.bfloat16


def iota(shape, dim):
    return lax.broadcasted_iota(jnp.int32, shape, dim)


def mm(a, b):
    return jnp.dot(a, b, preferred_element_type=F32)


def mm_nt(a, b):
    return lax.dot_general(a, b, (((1,), (1,)), ((), ())), preferred_element_type=F32)


def mm_tn(a, b):
    return lax.dot_general(a, b, (((0,), (0,)), ((), ())), preferred_element_type=F32)


def softplus(v):
    return jnp.maximum(v, 0.0) + jnp.log1p(jnp.exp(-jnp.abs(v)))


def drain(blocks, sem):
    most = blocks.at[pl.ds(0, blocks.shape[0] - 1)]
    pltpu.make_async_copy(most, most, sem).wait()


def kernel(
    halo_hbm, unm_hbm, own_hbm, cand_hbm, len_hbm, pick_hbm, desc_hbm,
    out_ref, best_ref,
    halo_v, unm_v, own_v, cand_v, len_v, pick_v, desc_v,
    send_v, recv_v, meta_s, meta_r, reply_v, back_v, bmeta_s, bmeta_r, bests,
    put_v, take_v, merit_v, picked_v, fields_v, res_v,
    load_sem, desc_sem, dsend, drecv, rsend, rrecv, msend, mrecv, psend, precv, bsend, brecv, xsend, xrecv, self_sem, pair_sem,
):
    me = lax.axis_index("space")
    core = lax.axis_index("rep")
    other = 1 - core
    mz, my, mx = me // 16, (me // 4) % 4, me % 4

    loads = [
        pltpu.make_async_copy(own_hbm, own_v, load_sem.at[0]),
        pltpu.make_async_copy(halo_hbm, halo_v, load_sem.at[1]),
        pltpu.make_async_copy(cand_hbm.at[pl.ds(2 * core, 2)], cand_v, load_sem.at[2]),
        pltpu.make_async_copy(unm_hbm, unm_v, load_sem.at[3]),
        pltpu.make_async_copy(len_hbm, len_v, load_sem.at[4]),
        pltpu.make_async_copy(pick_hbm, pick_v, load_sem.at[5]),
    ]
    for load in loads:
        load.start()
    desc_load = pltpu.make_async_copy(
        desc_hbm.at[pl.ds(2 * core, 2)], desc_v.at[core], desc_sem
    )
    desc_load.start()

    barrier = pltpu.get_barrier_semaphore()

    def peer(dz, dy, dx):
        return ((mz + dz) % 8) * 16 + ((my + dy) % 4) * 4 + (mx + dx) % 4

    for step in (4, 3, 5, 2, 6, 1, 7, 0):
        for dy in (2, 1, 3, 0):
            for dx in (2, 1, 3, 0):
                if step or dy or dx:
                    pl.semaphore_signal(
                        barrier, inc=1, device_id=(peer(step, dy, dx), core), device_id_type=MESH
                    )
                else:
                    pl.semaphore_signal(
                        barrier, inc=1, device_id=(me, other), device_id_type=MESH
                    )

    for load in loads:
        load.wait()

    lane_h = iota((HALOS, HALOS), 1)
    sub_h = iota((HALOS, HALOS), 0)
    before = (sub_h < lane_h).astype(BF16)
    owners = own_v[...]
    hots, goals, ranks = [], [], []
    for snap in range(4):
        owner = owners[snap : snap + 1, :]
        hot = (sub_h == owner).astype(F32)
        hot16 = hot.astype(BF16)
        rank = jnp.sum(mm(hot16, before) * hot, axis=0, keepdims=True)
        hots.append(hot16)
        ranks.append(rank)
        goals.append(owner.astype(F32) * 4.0 + 2.0 * (snap % 2) + rank)
    row_id = iota((REQS, 2 * HALOS), 0).astype(F32)
    for pair in range(2):
        goal = jnp.concatenate([goals[2 * pair], goals[2 * pair + 1]], axis=1)
        put = (row_id == goal).astype(F32).astype(BF16)
        rows = halo_v[2 * pair : 2 * pair + 2].reshape(2 * HALOS, HALF)
        send_v[pair * PEERS : (pair + 1) * PEERS] = mm(put, rows).astype(BF16).reshape(PEERS, SLOTS, HALF)
        put_v[pair] = put

    first = core == 0
    own_hot = [jnp.where(first, hots[j].astype(F32), hots[2 + j].astype(F32)) for j in range(2)]
    own_rank = [jnp.where(first, ranks[j], ranks[2 + j]) for j in range(2)]
    spans = len_v[...]
    picks = pick_v[...]
    lives = unm_v[...]
    folded = jnp.zeros((PEERS, HALF), F32)
    lane = iota((HALOS, HALF), 1)
    spread = (iota((K, HALF), 1) % 32 == iota((K, HALF), 0)).astype(BF16)
    lane_k = iota((HALOS, K), 1).astype(F32)
    for j in range(2):
        def mine(a):
            return jnp.where(first, a[j : j + 1, :], a[2 + j : 3 + j, :]).astype(F32)
        span = jnp.where(mine(lives) == 1.0, mine(spans), 0.0)
        pick = jnp.where(mine(lives) == 1.0, mine(picks), -1.0)
        slot = own_rank[j] + 2.0 * j
        rows8 = jnp.concatenate([span, pick, slot, jnp.zeros((HALOS - 3, HALOS), F32)], axis=0)
        cols = rows8.T
        span_c, pick_c, slot_c = cols[:, 0:1], cols[:, 1:2], cols[:, 2:3]
        listed = cand_v[j].astype(F32)
        coded = listed - jnp.where(listed < 256.0, 256.0, 255.0)
        chosen = jnp.sum(jnp.where(lane_k == pick_c, coded, 0.0), axis=1, keepdims=True)
        coded = jnp.where(lane_k < span_c, coded, 0.0)
        wide = mm(coded.astype(BF16), spread)
        wide = jnp.where(lane % 32 == K, chosen, wide)
        wide = jnp.where((lane // 32).astype(F32) == slot_c, wide, 0.0)
        folded = folded + mm(own_hot[j].astype(BF16), wide.astype(BF16))
    meta_s[...] = folded.reshape(PEERS, 1, HALF)

    pl.semaphore_wait(barrier, PEERS)
    pl.semaphore_signal(pair_sem, inc=1, device_id=(me, other), device_id_type=MESH)
    pl.semaphore_wait(pair_sem, 1)

    desc_send = pltpu.make_async_remote_copy(
        src_ref=desc_hbm.at[pl.ds(2 * other, 2)], dst_ref=desc_v.at[core],
        send_sem=dsend, recv_sem=drecv, device_id=(me, other), device_id_type=MESH,
    )
    desc_send.start()

    def send_requests(step, carry):
        far = 127 - step
        goal = peer(far // 16, (far // 4) % 4, far % 4)
        pltpu.make_async_remote_copy(
            src_ref=meta_s.at[goal], dst_ref=meta_r.at[me],
            send_sem=msend, recv_sem=mrecv, device_id=(goal, core), device_id_type=MESH,
        ).start()
        for pair in range(2):
            pltpu.make_async_remote_copy(
                src_ref=send_v.at[pair * PEERS + goal], dst_ref=recv_v.at[core * PEERS + me],
                send_sem=rsend, recv_sem=rrecv, device_id=(goal, pair), device_id_type=MESH,
            ).start()
        return carry

    lax.fori_loop(0, PEERS - 1, send_requests, 0)
    pltpu.make_async_remote_copy(
        src_ref=send_v.at[other * PEERS + me], dst_ref=recv_v.at[core * PEERS + me],
        send_sem=rsend, recv_sem=rrecv, device_id=(me, other), device_id_type=MESH,
    ).start()
    self_row = pltpu.make_async_copy(send_v.at[core * PEERS + me], recv_v.at[core * PEERS + me], self_sem.at[0])
    self_meta = pltpu.make_async_copy(meta_s.at[me], meta_r.at[me], self_sem.at[1])
    self_row.start()
    self_meta.start()

    col_id = iota((2 * HALOS, REQS), 1).astype(F32)
    for pair in range(2):
        goal_rows = jnp.concatenate(
            [goals[2 * pair], goals[2 * pair + 1], jnp.zeros((HALOS - 2, HALOS), F32)], axis=0
        )
        live_rows = jnp.concatenate(
            [lives[2 * pair : 2 * pair + 2, :].astype(F32), jnp.zeros((HALOS - 2, HALOS), F32)], axis=0
        )
        goal_c, live_c = goal_rows.T, live_rows.T
        goal_c = jnp.concatenate([goal_c[:, 0:1], goal_c[:, 1:2]], axis=0)
        live_c = jnp.concatenate([live_c[:, 0:1], live_c[:, 1:2]], axis=0)
        take_v[pair] = jnp.where((col_id == goal_c) & (live_c == 1.0), 1.0, 0.0).astype(BF16)

    desc_load.wait()
    desc_send.wait()
    self_row.wait()
    self_meta.wait()

    drain(meta_r, mrecv)
    copies = (((iota((REQS, PEERS), 0) // SLOTS) == iota((REQS, PEERS), 1))).astype(BF16)
    spreadm = mm(copies, meta_r[...].reshape(PEERS, HALF).astype(BF16))
    mine_lane = (iota((REQS, HALF), 1) // 32) == (iota((REQS, HALF), 0) % SLOTS)
    fold = (iota((HALF, HALF), 0) % 32 == iota((HALF, HALF), 1)).astype(BF16)
    fields_v[...] = mm(jnp.where(mine_lane, spreadm, 0.0).astype(BF16), fold)

    drain(recv_v, rrecv)
    rows = [recv_v[part * PEERS : (part + 1) * PEERS].reshape(REQS, HALF) for part in range(2)]
    odd = ((iota((REQS, HALF), 0) // 2) % 2).astype(F32)
    odd16 = odd.astype(BF16)
    even16 = (1.0 - odd).astype(BF16)
    left = jnp.concatenate(
        [rows[0] * even16, rows[1] * even16, rows[0] * odd16, rows[1] * odd16], axis=1
    )
    right = jnp.concatenate(
        [desc_v[0, 0], desc_v[1, 0], desc_v[0, 1], desc_v[1, 1]], axis=1
    )
    merit_v[...] = mm_nt(left, right) * 0.0625

    cid = iota((1, CANDS), 1)
    code = (cid - jnp.where(cid < 256, 256, 255)).astype(F32)
    lane_r = iota((ROWS, HALF), 1)

    def rows_pass(block, col):
        at = pl.ds(pl.multiple_of(block * ROWS, ROWS), ROWS)
        merit = merit_v[at, :]
        field = fields_v[at, :]
        kept = jnp.full((ROWS, CANDS), NEG, F32)
        for k in range(K):
            kept = jnp.where(field[:, k : k + 1] == code, merit, kept)
        pick = field[:, K : K + 1] == code
        picked_v[at, :] = jnp.where(pick, 1.0, 0.0).astype(BF16)
        top = jnp.max(kept, axis=1, keepdims=True)
        got = jnp.max(jnp.where(pick, merit, NEG), axis=1, keepdims=True)
        res_v[at, :] = jnp.where(lane_r == 0, top, got)
        return jnp.maximum(col, jnp.max(kept.reshape(ROWS // 8, 8, CANDS), axis=0))

    col = lax.fori_loop(0, REQS // ROWS, rows_pass, jnp.full((8, CANDS), NEG, F32))
    col = jnp.maximum(col, pltpu.roll(col, 4, 0))
    sub = iota((8, CANDS), 0)
    swapped = jnp.where(sub % 2 == 0, pltpu.roll(col, 7, 0), pltpu.roll(col, 1, 0))
    col = jnp.maximum(col, swapped)
    col = jnp.concatenate([col, col], axis=0)

    def claim_pass(block, carry):
        at = pl.ds(pl.multiple_of(block * ROWS, ROWS), ROWS)
        pick = picked_v[at, :].astype(F32) > 0.5
        claim = jnp.max(jnp.where(pick, col, NEG), axis=1, keepdims=True)
        res_v[at, :] = jnp.where(lane_r == 2, claim, res_v[at, :])
        return carry

    lax.fori_loop(0, REQS // ROWS, claim_pass, 0)

    res = res_v[...]
    quality = 1.0 + softplus(res)
    mine_q, claim_q = quality[:, 1:2], quality[:, 2:3]
    share = mine_q / (mine_q + claim_q)
    picked = picked_v[...]
    for part in range(2):
        even_rows = mm(picked, desc_v[part, 0])
        odd_rows = mm(picked, desc_v[part, 1])
        found = jnp.where(odd == 0.0, even_rows, odd_rows)
        blend = (1.0 - share) * rows[part].astype(F32) + share * found
        reply_v[part * PEERS : (part + 1) * PEERS] = blend.astype(BF16).reshape(PEERS, SLOTS, HALF)
    tops = jnp.where(iota((REQS, HALF), 1) == iota((REQS, HALF), 0) % SLOTS, res[:, 0:1], 0.0)
    bmeta_s[...] = mm_tn(copies, tops.astype(BF16)).reshape(PEERS, 1, HALF)

    def send_replies(step, carry):
        far = 127 - step
        goal = peer(far // 16, (far // 4) % 4, far % 4)
        pltpu.make_async_remote_copy(
            src_ref=bmeta_s.at[goal], dst_ref=bmeta_r.at[me],
            send_sem=bsend, recv_sem=brecv, device_id=(goal, core), device_id_type=MESH,
        ).start()
        for part in range(2):
            pltpu.make_async_remote_copy(
                src_ref=reply_v.at[part * PEERS + goal], dst_ref=back_v.at[core * PEERS + me],
                send_sem=psend, recv_sem=precv, device_id=(goal, part), device_id_type=MESH,
            ).start()
        return carry

    lax.fori_loop(0, PEERS - 1, send_replies, 0)
    pltpu.make_async_remote_copy(
        src_ref=reply_v.at[other * PEERS + me], dst_ref=back_v.at[core * PEERS + me],
        send_sem=psend, recv_sem=precv, device_id=(me, other), device_id_type=MESH,
    ).start()
    self_back = pltpu.make_async_copy(reply_v.at[core * PEERS + me], back_v.at[core * PEERS + me], self_sem.at[0])
    self_best = pltpu.make_async_copy(bmeta_s.at[me], bmeta_r.at[me], self_sem.at[1])
    self_back.start()
    self_best.start()
    self_best.wait()

    drain(bmeta_r, brecv)
    tops_back = bmeta_r[...].reshape(PEERS, HALF).astype(BF16)
    best_rows = []
    for j in range(2):
        found = mm_tn(tops_back, own_hot[j].astype(BF16))
        value = jnp.where(own_rank[j] == 0.0, found[2 * j : 2 * j + 1, :], found[2 * j + 1 : 2 * j + 2, :])
        live = jnp.where(first, lives[j : j + 1, :], lives[2 + j : 3 + j, :])
        best_rows.append(jnp.where(live == 1, value, 0.0))
    bests[core] = jnp.concatenate(best_rows + [jnp.zeros((6, HALOS), F32)], axis=0)
    best_send = pltpu.make_async_remote_copy(
        src_ref=bests.at[core], dst_ref=bests.at[core],
        send_sem=xsend, recv_sem=xrecv, device_id=(me, other), device_id_type=MESH,
    )
    best_send.start()

    self_back.wait()
    drain(back_v, precv)
    for pair in range(2):
        live_rows = jnp.concatenate(
            [lives[2 * pair : 2 * pair + 2, :].astype(F32), jnp.zeros((HALOS - 2, HALOS), F32)], axis=0
        ).T
        live_c = jnp.concatenate([live_rows[:, 0:1], live_rows[:, 1:2]], axis=0)
        came = mm(take_v[pair], back_v[pair * PEERS : (pair + 1) * PEERS].reshape(REQS, HALF))
        kept = halo_v[2 * pair : 2 * pair + 2].reshape(2 * HALOS, HALF).astype(F32)
        out = jnp.where(live_c == 1.0, came, kept)
        out_ref[2 * pair : 2 * pair + 2] = out.astype(BF16).reshape(2, HALOS, HALF)
    best_send.wait()
    best_ref[...] = jnp.concatenate([bests[0, 0:2], bests[1, 0:2]], axis=0).astype(BF16)

    drain(send_v, rsend)
    drain(reply_v, psend)
    drain(meta_s, msend)
    drain(bmeta_s, bsend)


def body(halo_rows, unmatched, owner_id, cand_index, lengths, choice_index, desc_rows):
    any_space = pl.BlockSpec(memory_space=pl.ANY)
    vmem = pl.BlockSpec(memory_space=pltpu.VMEM)
    dma = pltpu.SemaphoreType.DMA
    return pl.pallas_call(
        kernel,
        name="phantom",
        out_shape=(
            jax.ShapeDtypeStruct(halo_rows.shape, BF16),
            jax.ShapeDtypeStruct(unmatched.shape, BF16),
        ),
        in_specs=[any_space] * 7,
        out_specs=(vmem, vmem),
        scratch_shapes=[
            pltpu.VMEM((4, HALOS, HALF), BF16),
            pltpu.VMEM((4, HALOS), jnp.int32),
            pltpu.VMEM((4, HALOS), jnp.int32),
            pltpu.VMEM((2, HALOS, K), jnp.int32),
            pltpu.VMEM((4, HALOS), jnp.int32),
            pltpu.VMEM((4, HALOS), jnp.int32),
            pltpu.VMEM((2, 2, CANDS, HALF), BF16),
            pltpu.VMEM((2 * PEERS, SLOTS, HALF), BF16),
            pltpu.VMEM((2 * PEERS, SLOTS, HALF), BF16),
            pltpu.VMEM((PEERS, 1, HALF), F32),
            pltpu.VMEM((PEERS, 1, HALF), F32),
            pltpu.VMEM((2 * PEERS, SLOTS, HALF), BF16),
            pltpu.VMEM((2 * PEERS, SLOTS, HALF), BF16),
            pltpu.VMEM((PEERS, 1, HALF), F32),
            pltpu.VMEM((PEERS, 1, HALF), F32),
            pltpu.VMEM((2, 8, HALOS), F32),
            pltpu.VMEM((2, REQS, 2 * HALOS), BF16),
            pltpu.VMEM((2, 2 * HALOS, REQS), BF16),
            pltpu.VMEM((REQS, CANDS), F32),
            pltpu.VMEM((REQS, CANDS), BF16),
            pltpu.VMEM((REQS, HALF), F32),
            pltpu.VMEM((REQS, HALF), F32),
            dma((6,)), dma, dma, dma, dma, dma, dma, dma, dma, dma, dma, dma, dma, dma, dma((2,)),
            pltpu.SemaphoreType.REGULAR,
        ],
        compiler_params=pltpu.CompilerParams(collective_id=0, has_side_effects=True),
    )(halo_rows, unmatched, owner_id[:, :, 0], cand_index, lengths, choice_index, desc_rows)


def solution(mesh):
    in_specs = (
        P(None, "space", "rep"),
        P(None, "space"),
        P(None, "space", None),
        P(None, "space", None),
        P(None, "space"),
        P(None, "space"),
        P(None, "space", "rep"),
    )
    out_specs = (P(None, "space", "rep"), P(None, "space"))
    return jax.shard_map(body, mesh=mesh, in_specs=in_specs, out_specs=out_specs, check_vma=False)
```

profile of v0, /device:TPU:1, one launch (start us, length us, event | category | flops | bytes accessed | tf_op | source)
XLA Modules:
  0.0 56.6 jit_solution(7671502812369131213)
XLA Ops:
  0.6 1.6 %copy.9.cand_hbm = s32[4,128,16]{2,1,0:T(8,128)} copy(s32[4,128,16]{1,2,0:T(8,128)} %param.10) | data formatting | bytes 65536 | tf_op args[3]
  2.2 52.2 %phantom.1 = (bf16[4,128,128]{2,1,0:T(8,128)(2,1)}, bf16[4,128]{1,0:T(4,128)(2,1)}) custom-call(bf16[4,128,128]{2,1,0:T(8,128)(2,1)} %halo_hbm.1, s32[4,128]{1,0:T(4,128)} %unm_hbm.1, s32[4,128]{1,0:T(4,128)} %bitcast.1, s32[4,128,16]{2,1,0:T(8,128)} %copy.9.cand_hbm, s32[4,128]{1,0:T(4,128)} %len_hbm.1, s32[4,128]{1,0:T(4,128)} %pick_hbm.1, ...), custom_call_target="tpu_custom_call" | custom-call | tf_op jit(solution)/shard_map/phantom/pallas_call | solution.py:329
  54.5 0.0 copy-start
  54.5 1.6 %copy.12 = bf16[4,128,128]{2,1,0:T(8,128)(2,1)} copy(bf16[4,128,128]{2,1,0:T(8,128)(2,1)} %get-tuple-element.4) | data formatting | bytes 262144
  56.0 0.0 copy-done
  56.0 0.6 copy.13
Async XLA Ops:
  54.5 1.6 %copy-start = (bf16[4,128]{1,0:T(4,128)(2,1)S(1)}, bf16[4,128]{1,0:T(4,128)(2,1)}, u32[]{:S(2)}) copy-start(bf16[4,128]{1,0:T(4,128)(2,1)} %get-tuple-element.5) | copy-start | bytes 3076
where the time goes:
time: 56.8 us; the launch traced here: 56.6 us
  Pallas kernels  52.2 us (92%)
  local copies, waits for them, and re-layouts  3.71 us (7%)
  between operations  0.65 us (1%)
    pallas_call x1, Pallas kernels, body(): pl.pallas_call(kernel, name='phantom', out_shape=(jax.ShapeDtypeStruct(ha...  52.2 us
    unnamed x5, local copies, waits for them, and re-layouts  3.71 us

commit v1 on v0

v1 whole, which is shorter than its diff:
```python
import jax
import jax.numpy as jnp
from jax import lax
from jax.experimental import pallas as pl
from jax.experimental.pallas import tpu as pltpu
from jax.sharding import PartitionSpec as P

MESH = pl.DeviceIdType.MESH
PEERS = 128
HALOS = 128
CANDS = 512
SLOTS = 4
REQS = PEERS * SLOTS
HALF = 128
K = 16
ROWS = 16
PLANE = 16 * SLOTS
NEG = -1e30
F32 = jnp.float32
BF16 = jnp.bfloat16


def iota(shape, dim):
    return lax.broadcasted_iota(jnp.int32, shape, dim)


def mm(a, b):
    return jnp.dot(a, b, preferred_element_type=F32)


def mm_nt(a, b):
    return lax.dot_general(a, b, (((1,), (1,)), ((), ())), preferred_element_type=F32)


def mm_tn(a, b):
    return lax.dot_general(a, b, (((0,), (0,)), ((), ())), preferred_element_type=F32)


def softplus(v):
    return jnp.maximum(v, 0.0) + jnp.log1p(jnp.exp(-jnp.abs(v)))


def drain(blocks, sem):
    most = blocks.at[pl.ds(0, blocks.shape[0] - 1)]
    pltpu.make_async_copy(most, most, sem).wait()


def kernel(
    halo_hbm, unm_hbm, own_hbm, cand_hbm, len_hbm, pick_hbm, desc_hbm,
    out_ref, best_ref,
    halo_v, unm_v, own_v, cand_v, len_v, pick_v, desc_v, right_v,
    send_v, recv_v, meta_s, meta_r, reply_v, back_v, bmeta_s, bmeta_r, bests,
    put_v, take_v, merit_v, picked_v, fields_v, res_v, found_v,
    load_sem, desc_sem, dsend, drecv, rsend, rrecv, msend, mrecv, psend, precv, bsend, brecv, xsend, xrecv, pair_sem,
):
    me = lax.axis_index("space")
    core = lax.axis_index("rep")
    other = 1 - core
    mz, my, mx = me // 16, (me // 4) % 4, me % 4

    loads = [
        pltpu.make_async_copy(own_hbm, own_v, load_sem.at[0]),
        pltpu.make_async_copy(halo_hbm, halo_v, load_sem.at[1]),
        pltpu.make_async_copy(cand_hbm.at[pl.ds(2 * core, 2)], cand_v, load_sem.at[2]),
        pltpu.make_async_copy(unm_hbm, unm_v, load_sem.at[3]),
        pltpu.make_async_copy(len_hbm, len_v, load_sem.at[4]),
        pltpu.make_async_copy(pick_hbm, pick_v, load_sem.at[5]),
    ]
    for load in loads:
        load.start()
    desc_load = pltpu.make_async_copy(
        desc_hbm.at[pl.ds(2 * core, 2)], desc_v.at[core], desc_sem
    )
    desc_load.start()

    barrier = pltpu.get_barrier_semaphore()
    in_plane = [((my + dy) % 4) * 4 + (mx + dx) % 4 for dy in (2, 1, 3, 0) for dx in (2, 1, 3, 0)]
    for dz in (4, 3, 5, 2, 6, 1, 7, 0):
        plane = ((mz + dz) % 8) * 16
        for spot in range(16):
            if dz or spot < 15:
                goal = (plane + in_plane[spot], core)
            else:
                goal = (me, other)
            pl.semaphore_signal(barrier, inc=1, device_id=goal, device_id_type=MESH)

    for load in loads:
        load.wait()

    lane_h = iota((HALOS, HALOS), 1)
    sub_h = iota((HALOS, HALOS), 0)
    before = (sub_h < lane_h).astype(BF16)
    owners = own_v[...]
    hots, goals, ranks = [], [], []
    for snap in range(4):
        owner = owners[snap : snap + 1, :]
        hot = (sub_h == owner).astype(F32)
        rank = jnp.sum(mm(hot.astype(BF16), before) * hot, axis=0, keepdims=True)
        hots.append(hot)
        ranks.append(rank)
        goals.append(owner.astype(F32) * 4.0 + 2.0 * (snap % 2) + rank)
    row_id = iota((REQS, 2 * HALOS), 0).astype(F32)
    for pair in range(2):
        goal = jnp.concatenate([goals[2 * pair], goals[2 * pair + 1]], axis=1)
        put = (row_id == goal).astype(F32).astype(BF16)
        rows = halo_v[2 * pair : 2 * pair + 2].reshape(2 * HALOS, HALF)
        send_v[pair * PEERS : (pair + 1) * PEERS] = mm(put, rows).astype(BF16).reshape(PEERS, SLOTS, HALF)

    first = core == 0
    own_hot = [jnp.where(first, hots[j], hots[2 + j]).astype(BF16) for j in range(2)]
    own_rank = [jnp.where(first, ranks[j], ranks[2 + j]) for j in range(2)]
    spans, picks, lives = len_v[...], pick_v[...], unm_v[...]
    folded = jnp.zeros((PEERS, HALF), F32)
    place = iota((K, HALOS), 0)
    for j in range(2):
        def mine(a):
            return jnp.where(first, a[j : j + 1, :], a[2 + j : 3 + j, :])
        span = jnp.where(mine(lives) == 1, mine(spans), 0)
        pick = jnp.where(mine(lives) == 1, mine(picks), -1)
        slot = own_rank[j] + 2.0 * j
        listed = cand_v[j]
        coded = (listed - jnp.where(listed < 256, 256, 255)).astype(F32)
        chosen = jnp.sum(jnp.where(place == pick, coded, 0.0), axis=0, keepdims=True)
        coded = jnp.where(place < span, coded, 0.0)
        tail = jnp.where(place == 0, chosen, 0.0)
        field = jnp.concatenate([coded, tail] * SLOTS, axis=0)
        field = jnp.where((sub_h // 32).astype(F32) == slot, field, 0.0)
        folded = folded + mm_nt(own_hot[j], field.astype(BF16))
    meta_s[...] = folded.reshape(PEERS, 1, HALF)

    pl.semaphore_wait(barrier, PEERS)
    pl.semaphore_signal(pair_sem, inc=1, device_id=(me, other), device_id_type=MESH)

    desc_send = pltpu.make_async_remote_copy(
        src_ref=desc_hbm.at[pl.ds(2 * other, 2)], dst_ref=desc_v.at[core],
        send_sem=dsend, recv_sem=drecv, device_id=(me, other), device_id_type=MESH,
    )
    desc_send.start()

    def reach(step):
        return 4 + (1 - 2 * (step % 2)) * ((step + 1) // 2)

    def remote(src, dst, send_sem, recv_sem, goal):
        pltpu.make_async_remote_copy(
            src_ref=src, dst_ref=dst, send_sem=send_sem, recv_sem=recv_sem,
            device_id=goal, device_id_type=MESH,
        ).start()

    def send_requests(step, carry):
        plane = ((mz + reach(step)) % 8) * 16
        for spot in range(15):
            goal = plane + in_plane[spot]
            remote(meta_s.at[goal], meta_r.at[me], msend, mrecv.at[step], (goal, core))
            remote(send_v.at[core * PEERS + goal], recv_v.at[core * PEERS + me], rsend, rrecv.at[step], (goal, core))

        @pl.when(step < 7)
        def _():
            goal = plane + in_plane[15]
            remote(meta_s.at[goal], meta_r.at[me], msend, mrecv.at[step], (goal, core))
            remote(send_v.at[core * PEERS + goal], recv_v.at[core * PEERS + me], rsend, rrecv.at[step], (goal, core))

        @pl.when(step == 0)
        def _():
            pl.semaphore_wait(pair_sem, 1)

        for spot in range(16):
            goal = plane + in_plane[spot]
            remote(send_v.at[other * PEERS + goal], recv_v.at[core * PEERS + me], rsend, rrecv.at[step], (goal, other))
        return carry

    lax.fori_loop(0, 8, send_requests, 0)
    self_row = pltpu.make_async_copy(send_v.at[core * PEERS + me], recv_v.at[core * PEERS + me], rrecv.at[7])
    self_meta = pltpu.make_async_copy(meta_s.at[me], meta_r.at[me], mrecv.at[7])
    self_row.start()
    self_meta.start()

    col_id = iota((2 * HALOS, REQS), 1).astype(F32)
    live_cols = []
    for pair in range(2):
        lists = jnp.concatenate(
            [goals[2 * pair], goals[2 * pair + 1], lives[2 * pair : 2 * pair + 2, :].astype(F32),
             jnp.zeros((HALOS - 4, HALOS), F32)], axis=0,
        ).T
        goal_c = jnp.concatenate([lists[:, 0:1], lists[:, 1:2]], axis=0)
        live_c = jnp.concatenate([lists[:, 2:3], lists[:, 3:4]], axis=0)
        take_v[pair] = jnp.where(col_id == goal_c, live_c, 0.0).astype(BF16)
        put_v[pair] = jnp.broadcast_to(live_c, (2 * HALOS, HALF))

    desc_load.wait()
    desc_send.wait()
    for snap in range(2):
        for part in range(2):
            right_v[(2 * snap + part) * HALF : (2 * snap + part + 1) * HALF, :] = desc_v[part, snap].T

    cid = iota((1, CANDS), 1)
    code = (cid - jnp.where(cid < 256, 256, 255)).astype(F32)
    lane_r = iota((ROWS, HALF), 1)
    odd = ((iota((PLANE, HALF), 0) // 2) % 2).astype(F32)
    odd16 = odd.astype(BF16)
    even16 = (1.0 - odd).astype(BF16)
    lane_p = iota((16, HALF), 1)

    def score_plane(step, col):
        back = ((mz + 8 - reach(step)) % 8) * 16
        base = pl.multiple_of(back * SLOTS, PLANE)
        at = pl.ds(base, PLANE)
        pltpu.make_async_copy(meta_r.at[pl.ds(0, 16)], meta_r.at[pl.ds(0, 16)], mrecv.at[step]).wait()
        got = meta_r[pl.ds(back, 16)].reshape(16, HALF)
        for slot in range(SLOTS):
            moved = got if slot == 0 else pltpu.roll(got, HALF - 32 * slot, 1)
            fields_v[pl.ds(base + slot, 16, stride=SLOTS), :] = moved
        pltpu.make_async_copy(recv_v.at[pl.ds(0, 32)], recv_v.at[pl.ds(0, 32)], rrecv.at[step]).wait()
        rows = [recv_v[pl.ds(part * PEERS + back, 16)].reshape(PLANE, HALF) for part in range(2)]
        left = jnp.concatenate(
            [rows[0] * even16, rows[1] * even16, rows[0] * odd16, rows[1] * odd16], axis=1
        )
        merit_v[...] = mm(left, right_v[...]) * 0.0625
        for block in range(PLANE // ROWS):
            here = pl.ds(block * ROWS, ROWS)
            there = pl.ds(pl.multiple_of(base + block * ROWS, ROWS), ROWS)
            merit = merit_v[here, :]
            field = fields_v[there, :]
            kept = jnp.full((ROWS, CANDS), NEG, F32)
            for k in range(K):
                kept = jnp.where(field[:, k : k + 1] == code, merit, kept)
            pick = field[:, K : K + 1] == code
            picked_v[there, :] = jnp.where(pick, 1.0, 0.0).astype(BF16)
            top = jnp.max(kept, axis=1, keepdims=True)
            got_merit = jnp.max(jnp.where(pick, merit, NEG), axis=1, keepdims=True)
            res_v[there, :] = jnp.where(lane_r < 64, top, got_merit)
            col = jnp.maximum(col, jnp.max(kept.reshape(ROWS // 8, 8, CANDS), axis=0))
        picked = picked_v[at, :]
        for part in range(2):
            even_rows = mm(picked, desc_v[part, 0])
            odd_rows = mm(picked, desc_v[part, 1])
            found_v[at, part * HALF : (part + 1) * HALF] = jnp.where(odd == 0.0, even_rows, odd_rows)
        tops = jnp.zeros((16, HALF), F32)
        for slot in range(SLOTS):
            tops = jnp.where(lane_p == slot, res_v[pl.ds(base + slot, 16, stride=SLOTS), :], tops)
        bmeta_s[pl.ds(back, 16)] = tops.reshape(16, 1, HALF)
        for spot in range(15):
            goal = back + in_plane[spot]
            remote(bmeta_s.at[goal], bmeta_r.at[me], bsend, brecv, (goal, core))

        @pl.when(step < 7)
        def _():
            goal = back + in_plane[15]
            remote(bmeta_s.at[goal], bmeta_r.at[me], bsend, brecv, (goal, core))

        return col

    col = lax.fori_loop(0, 8, score_plane, jnp.full((8, CANDS), NEG, F32))
    col = jnp.maximum(col, pltpu.roll(col, 4, 0))
    sub = iota((8, CANDS), 0)
    swapped = jnp.where(sub % 2 == 0, pltpu.roll(col, 7, 0), pltpu.roll(col, 1, 0))
    col = jnp.maximum(col, swapped)
    col = jnp.concatenate([col] * (PLANE // 8), axis=0)

    def reply_plane(step, carry):
        back = ((mz + 8 - reach(step)) % 8) * 16
        at = pl.ds(pl.multiple_of(back * SLOTS, PLANE), PLANE)
        pick = fields_v[at, :][:, K : K + 1] == code
        claim = jnp.max(jnp.where(pick, col, NEG), axis=1, keepdims=True)
        quality = 1.0 + softplus(jnp.where(iota((PLANE, HALF), 1) < 64, claim, res_v[at, :]))
        claim_q, mine_q = quality[:, 0:1], quality[:, 64:65]
        share = mine_q / (mine_q + claim_q)
        for part in range(2):
            blocks = pl.ds(part * PEERS + back, 16)
            row = recv_v[blocks].reshape(PLANE, HALF).astype(F32)
            blend = (1.0 - share) * row + share * found_v[at, part * HALF : (part + 1) * HALF]
            reply_v[blocks] = blend.astype(BF16).reshape(16, SLOTS, HALF)
        for spot in range(16):
            goal = back + in_plane[spot]
            remote(reply_v.at[other * PEERS + goal], back_v.at[core * PEERS + me], psend, precv, (goal, other))
        for spot in range(15):
            goal = back + in_plane[spot]
            remote(reply_v.at[core * PEERS + goal], back_v.at[core * PEERS + me], psend, precv, (goal, core))

        @pl.when(step < 7)
        def _():
            goal = back + in_plane[15]
            remote(reply_v.at[core * PEERS + goal], back_v.at[core * PEERS + me], psend, precv, (goal, core))

        return carry

    lax.fori_loop(0, 8, reply_plane, 0)
    self_back = pltpu.make_async_copy(reply_v.at[core * PEERS + me], back_v.at[core * PEERS + me], load_sem.at[0])
    self_best = pltpu.make_async_copy(bmeta_s.at[me], bmeta_r.at[me], load_sem.at[1])
    self_back.start()
    self_best.start()
    self_best.wait()
    drain(bmeta_r, brecv)
    tops_back = bmeta_r[...].reshape(PEERS, HALF).astype(BF16)
    best_rows = []
    for j in range(2):
        found = mm_tn(tops_back, own_hot[j])
        value = jnp.where(own_rank[j] == 0.0, found[2 * j : 2 * j + 1, :], found[2 * j + 1 : 2 * j + 2, :])
        live = jnp.where(first, lives[j : j + 1, :], lives[2 + j : 3 + j, :])
        best_rows.append(jnp.where(live == 1, value, 0.0))
    bests[core] = jnp.concatenate(best_rows + [jnp.zeros((6, HALOS), F32)], axis=0)
    best_send = pltpu.make_async_remote_copy(
        src_ref=bests.at[core], dst_ref=bests.at[core],
        send_sem=xsend, recv_sem=xrecv, device_id=(me, other), device_id_type=MESH,
    )
    best_send.start()
    drain(send_v, rsend)
    drain(meta_s, msend)
    drain(bmeta_s, bsend)
    best_send.wait()
    best_ref[...] = jnp.concatenate([bests[0, 0:2], bests[1, 0:2]], axis=0).astype(BF16)

    self_back.wait()
    drain(back_v, precv)
    for pair in range(2):
        came = mm(take_v[pair], back_v[pair * PEERS : (pair + 1) * PEERS].reshape(REQS, HALF))
        kept = halo_v[2 * pair : 2 * pair + 2].reshape(2 * HALOS, HALF).astype(F32)
        out = jnp.where(put_v[pair] == 1.0, came, kept)
        out_ref[2 * pair : 2 * pair + 2] = out.astype(BF16).reshape(2, HALOS, HALF)
    drain(reply_v, psend)


def body(halo_rows, unmatched, owner_id, cand_index, lengths, choice_index, desc_rows):
    any_space = pl.BlockSpec(memory_space=pl.ANY)
    vmem = pl.BlockSpec(memory_space=pltpu.VMEM)
    dma = pltpu.SemaphoreType.DMA
    return pl.pallas_call(
        kernel,
        name="phantom",
        out_shape=(
            jax.ShapeDtypeStruct(halo_rows.shape, BF16),
            jax.ShapeDtypeStruct(unmatched.shape, BF16),
        ),
        in_specs=[any_space] * 7,
        out_specs=(vmem, vmem),
        scratch_shapes=[
            pltpu.VMEM((4, HALOS, HALF), BF16),
            pltpu.VMEM((4, HALOS), jnp.int32),
            pltpu.VMEM((4, HALOS), jnp.int32),
            pltpu.VMEM((2, K, HALOS), jnp.int32),
            pltpu.VMEM((4, HALOS), jnp.int32),
            pltpu.VMEM((4, HALOS), jnp.int32),
            pltpu.VMEM((2, 2, CANDS, HALF), BF16),
            pltpu.VMEM((4 * HALF, CANDS), BF16),
            pltpu.VMEM((2 * PEERS, SLOTS, HALF), BF16),
            pltpu.VMEM((2 * PEERS, SLOTS, HALF), BF16),
            pltpu.VMEM((PEERS, 1, HALF), F32),
            pltpu.VMEM((PEERS, 1, HALF), F32),
            pltpu.VMEM((2 * PEERS, SLOTS, HALF), BF16),
            pltpu.VMEM((2 * PEERS, SLOTS, HALF), BF16),
            pltpu.VMEM((PEERS, 1, HALF), F32),
            pltpu.VMEM((PEERS, 1, HALF), F32),
            pltpu.VMEM((2, 8, HALOS), F32),
            pltpu.VMEM((2, 2 * HALOS, HALF), F32),
            pltpu.VMEM((2, 2 * HALOS, REQS), BF16),
            pltpu.VMEM((PLANE, CANDS), F32),
            pltpu.VMEM((REQS, CANDS), BF16),
            pltpu.VMEM((REQS, HALF), F32),
            pltpu.VMEM((REQS, HALF), F32),
            pltpu.VMEM((REQS, 2 * HALF), F32),
            dma((6,)), dma, dma, dma, dma, dma((8,)), dma, dma((8,)), dma, dma, dma, dma, dma, dma,
            pltpu.SemaphoreType.REGULAR,
        ],
        compiler_params=pltpu.CompilerParams(collective_id=0, has_side_effects=True),
    )(halo_rows, unmatched, owner_id[:, :, 0], jnp.swapaxes(cand_index, 1, 2), lengths, choice_index, desc_rows)


def solution(mesh):
    in_specs = (
        P(None, "space", "rep"),
        P(None, "space"),
        P(None, "space", None),
        P(None, "space", None),
        P(None, "space"),
        P(None, "space"),
        P(None, "space", "rep"),
    )
    out_specs = (P(None, "space", "rep"), P(None, "space"))
    return jax.shard_map(body, mesh=mesh, in_specs=in_specs, out_specs=out_specs, check_vma=False)
```

time: 56.8 us -> 42.8 us (0.75)
  Pallas kernels: 52.2 us -> 39.9 us
  local copies, waits for them, and re-layouts: 3.71 us -> 2.14 us
    pallas_call x1, Pallas kernels: 52.2 us -> 39.9 us  [body(): pl.pallas_call(kernel, name='phantom', out_shape=(jax.ShapeDtypeStruct(ha...]
    unnamed x5 -> x4, local copies, waits for them, and re-layouts: 3.71 us -> 2.14 us
where the time goes in v1:
time: 42.8 us; the launch traced here: 42.7 us
  Pallas kernels  39.9 us (93%)
  local copies, waits for them, and re-layouts  2.14 us (5%)
  between operations  0.65 us (2%)
    pallas_call x1, Pallas kernels, body(): pl.pallas_call(kernel, name='phantom', out_shape=(jax.ShapeDtypeStruct(ha...  39.9 us
    unnamed x4, local copies, waits for them, and re-layouts  2.14 us

profile of v1, /device:TPU:1, one launch (start us, length us, event | category | flops | bytes accessed | tf_op | source)
XLA Modules:
  0.0 42.7 jit_solution(4123221589755502321)
XLA Ops:
  0.6 39.9 %phantom.1 = (bf16[4,128,128]{2,1,0:T(8,128)(2,1)}, bf16[4,128]{1,0:T(4,128)(2,1)}) custom-call(bf16[4,128,128]{2,1,0:T(8,128)(2,1)} %halo_hbm.1, s32[4,128]{1,0:T(4,128)} %unm_hbm.1, s32[4,128]{1,0:T(4,128)} %bitcast.3, s32[4,16,128]{2,1,0:T(8,128)} %bitcast.2, s32[4,128]{1,0:T(4,128)} %len_hbm.1, s32[4,128]{1,0:T(4,128)} %pick_hbm.1, ...), custom_call_target="tpu_custom_call" | custom-call | tf_op jit(solution)/shard_map/phantom/pallas_call | solution.py:326
  40.6 0.0 copy-start
  40.6 1.6 %copy.11 = bf16[4,128,128]{2,1,0:T(8,128)(2,1)} copy(bf16[4,128,128]{2,1,0:T(8,128)(2,1)} %get-tuple-element.4) | data formatting | bytes 262144
  42.2 0.0 copy-done
  42.2 0.6 %copy.12 = bf16[4,128]{1,0:T(4,128)(2,1)} copy(bf16[4,128]{1,0:T(4,128)(2,1)S(1)} %copy-done) | data formatting | bytes 2048
Async XLA Ops:
  40.6 1.6 %copy-start = (bf16[4,128]{1,0:T(4,128)(2,1)S(1)}, bf16[4,128]{1,0:T(4,128)(2,1)}, u32[]{:S(2)}) copy-start(bf16[4,128]{1,0:T(4,128)(2,1)} %get-tuple-element.5) | copy-start | bytes 3076

commit v2 on v1

--- a/solution.py
+++ b/solution.py
@@ -50,7 +50,7 @@
     out_ref, best_ref,
     halo_v, unm_v, own_v, cand_v, len_v, pick_v, desc_v, right_v,
     send_v, recv_v, meta_s, meta_r, reply_v, back_v, bmeta_s, bmeta_r, bests,
-    put_v, take_v, merit_v, picked_v, fields_v, res_v, found_v,
+    put_v, take_v, merit_v, picked_v, fields_v, res_v, found_v, shut_v,
     load_sem, desc_sem, dsend, drecv, rsend, rrecv, msend, mrecv, psend, precv, bsend, brecv, xsend, xrecv, pair_sem,
 ):
     me = lax.axis_index("space")
@@ -146,28 +146,37 @@
             device_id=goal, device_id_type=MESH,
         ).start()
 
+    def send_lists(step, carry):
+        plane = ((mz + reach(step)) % 8) * 16
+        for spot in range(15):
+            goal = plane + in_plane[spot]
+            remote(meta_s.at[goal], meta_r.at[me], msend, mrecv.at[step], (goal, core))
+
+        @pl.when(step < 7)
+        def _():
+            goal = plane + in_plane[15]
+            remote(meta_s.at[goal], meta_r.at[me], msend, mrecv.at[step], (goal, core))
+
+        return carry
+
     def send_requests(step, carry):
         plane = ((mz + reach(step)) % 8) * 16
         for spot in range(15):
             goal = plane + in_plane[spot]
-            remote(meta_s.at[goal], meta_r.at[me], msend, mrecv.at[step], (goal, core))
             remote(send_v.at[core * PEERS + goal], recv_v.at[core * PEERS + me], rsend, rrecv.at[step], (goal, core))
 
         @pl.when(step < 7)
         def _():
             goal = plane + in_plane[15]
-            remote(meta_s.at[goal], meta_r.at[me], msend, mrecv.at[step], (goal, core))
             remote(send_v.at[core * PEERS + goal], recv_v.at[core * PEERS + me], rsend, rrecv.at[step], (goal, core))
-
-        @pl.when(step == 0)
-        def _():
-            pl.semaphore_wait(pair_sem, 1)
 
         for spot in range(16):
             goal = plane + in_plane[spot]
             remote(send_v.at[other * PEERS + goal], recv_v.at[core * PEERS + me], rsend, rrecv.at[step], (goal, other))
         return carry
 
+    lax.fori_loop(0, 8, send_lists, 0)
+    pl.semaphore_wait(pair_sem, 1)
     lax.fori_loop(0, 8, send_requests, 0)
     self_row = pltpu.make_async_copy(send_v.at[core * PEERS + me], recv_v.at[core * PEERS + me], rrecv.at[7])
     self_meta = pltpu.make_async_copy(meta_s.at[me], meta_r.at[me], mrecv.at[7])
@@ -200,7 +209,8 @@
     even16 = (1.0 - odd).astype(BF16)
     lane_p = iota((16, HALF), 1)
 
-    def score_plane(step, col):
+    def list_plane(turn, carry):
+        step = 7 - turn
         back = ((mz + 8 - reach(step)) % 8) * 16
         base = pl.multiple_of(back * SLOTS, PLANE)
         at = pl.ds(base, PLANE)
@@ -209,31 +219,43 @@
         for slot in range(SLOTS):
             moved = got if slot == 0 else pltpu.roll(got, HALF - 32 * slot, 1)
             fields_v[pl.ds(base + slot, 16, stride=SLOTS), :] = moved
+        for block in range(PLANE // ROWS):
+            there = pl.ds(pl.multiple_of(base + block * ROWS, ROWS), ROWS)
+            field = fields_v[there, :]
+            shut = jnp.full((ROWS, CANDS), NEG, F32)
+            for k in range(K):
+                shut = jnp.where(field[:, k : k + 1] == code, 0.0, shut)
+            shut_v[there, :] = shut
+            pick = field[:, K : K + 1] == code
+            picked_v[there, :] = jnp.where(pick, 1.0, 0.0).astype(BF16)
+        picked = picked_v[at, :]
+        for part in range(2):
+            even_rows = mm(picked, desc_v[part, 0])
+            odd_rows = mm(picked, desc_v[part, 1])
+            found_v[at, part * HALF : (part + 1) * HALF] = jnp.where(odd == 0.0, even_rows, odd_rows)
+        return carry
+
+    lax.fori_loop(0, 8, list_plane, 0)
+
+    def score_plane(step, col):
+        back = ((mz + 8 - reach(step)) % 8) * 16
+        base = pl.multiple_of(back * SLOTS, PLANE)
+        at = pl.ds(base, PLANE)
         pltpu.make_async_copy(recv_v.at[pl.ds(0, 32)], recv_v.at[pl.ds(0, 32)], rrecv.at[step]).wait()
         rows = [recv_v[pl.ds(part * PEERS + back, 16)].reshape(PLANE, HALF) for part in range(2)]
         left = jnp.concatenate(
             [rows[0] * even16, rows[1] * even16, rows[0] * odd16, rows[1] * odd16], axis=1
         )
-        merit_v[...] = mm(left, right_v[...]) * 0.0625
+        merit_v[...] = mm(left, right_v[...])
+        product = rows[0].astype(F32) * found_v[at, 0:HALF] + rows[1].astype(F32) * found_v[at, HALF : 2 * HALF]
+        own_merit = jnp.sum(product, axis=1, keepdims=True)
         for block in range(PLANE // ROWS):
             here = pl.ds(block * ROWS, ROWS)
             there = pl.ds(pl.multiple_of(base + block * ROWS, ROWS), ROWS)
-            merit = merit_v[here, :]
-            field = fields_v[there, :]
-            kept = jnp.full((ROWS, CANDS), NEG, F32)
-            for k in range(K):
-                kept = jnp.where(field[:, k : k + 1] == code, merit, kept)
-            pick = field[:, K : K + 1] == code
-            picked_v[there, :] = jnp.where(pick, 1.0, 0.0).astype(BF16)
+            kept = merit_v[here, :] + shut_v[there, :]
             top = jnp.max(kept, axis=1, keepdims=True)
-            got_merit = jnp.max(jnp.where(pick, merit, NEG), axis=1, keepdims=True)
-            res_v[there, :] = jnp.where(lane_r < 64, top, got_merit)
+            res_v[there, :] = jnp.where(lane_r < 64, top, own_merit[block * ROWS : (block + 1) * ROWS]) * 0.0625
             col = jnp.maximum(col, jnp.max(kept.reshape(ROWS // 8, 8, CANDS), axis=0))
-        picked = picked_v[at, :]
-        for part in range(2):
-            even_rows = mm(picked, desc_v[part, 0])
-            odd_rows = mm(picked, desc_v[part, 1])
-            found_v[at, part * HALF : (part + 1) * HALF] = jnp.where(odd == 0.0, even_rows, odd_rows)
         tops = jnp.zeros((16, HALF), F32)
         for slot in range(SLOTS):
             tops = jnp.where(lane_p == slot, res_v[pl.ds(base + slot, 16, stride=SLOTS), :], tops)
@@ -249,7 +271,7 @@
 
         return col
 
-    col = lax.fori_loop(0, 8, score_plane, jnp.full((8, CANDS), NEG, F32))
+    col = lax.fori_loop(0, 8, score_plane, jnp.full((8, CANDS), NEG, F32)) * 0.0625
     col = jnp.maximum(col, pltpu.roll(col, 4, 0))
     sub = iota((8, CANDS), 0)
     swapped = jnp.where(sub % 2 == 0, pltpu.roll(col, 7, 0), pltpu.roll(col, 1, 0))
@@ -327,8 +349,8 @@
         kernel,
         name="phantom",
         out_shape=(
-            jax.ShapeDtypeStruct(halo_rows.shape, BF16),
-            jax.ShapeDtypeStruct(unmatched.shape, BF16),
+            pltpu.VMEM(halo_rows.shape, BF16),
+            pltpu.VMEM(unmatched.shape, BF16),
         ),
         in_specs=[any_space] * 7,
         out_specs=(vmem, vmem),
@@ -357,6 +379,7 @@
             pltpu.VMEM((REQS, HALF), F32),
             pltpu.VMEM((REQS, HALF), F32),
             pltpu.VMEM((REQS, 2 * HALF), F32),
+            pltpu.VMEM((REQS, CANDS), F32),
             dma((6,)), dma, dma, dma, dma, dma((8,)), dma, dma((8,)), dma, dma, dma, dma, dma, dma,
             pltpu.SemaphoreType.REGULAR,
         ],

time: 42.8 us -> 39.7 us (0.928)
  Pallas kernels: 39.9 us -> 37.8 us
  local copies, waits for them, and re-layouts: 2.14 us -> 1.22 us
    pallas_call x1, Pallas kernels: 39.9 us -> 37.8 us  [body(): pl.pallas_call(kernel, name='phantom', out_shape=(pltpu.VMEM(halo_rows.sh...]
    unnamed x4 -> x2, local copies, waits for them, and re-layouts: 2.14 us -> 1.22 us
where the time goes in v2:
time: 39.7 us; the launch traced here: 39.6 us
  Pallas kernels  37.8 us (95%)
  local copies, waits for them, and re-layouts  1.22 us (3%)
  between operations  0.64 us (2%)
    pallas_call x1, Pallas kernels, body(): pl.pallas_call(kernel, name='phantom', out_shape=(pltpu.VMEM(halo_rows.sh...  37.8 us
    unnamed x2, local copies, waits for them, and re-layouts  1.22 us

profile of v2, /device:TPU:1, one launch (start us, length us, event | category | flops | bytes accessed | tf_op | source)
XLA Modules:
  0.0 39.6 jit_solution(12756921585122940356)
XLA Ops:
  0.6 37.8 %phantom.1 = (bf16[4,128,128]{2,1,0:T(8,128)(2,1)S(1)}, bf16[4,128]{1,0:T(4,128)(2,1)S(1)}) custom-call(bf16[4,128,128]{2,1,0:T(8,128)(2,1)} %halo_hbm.1, s32[4,128]{1,0:T(4,128)} %unm_hbm.1, s32[4,128]{1,0:T(4,128)} %bitcast.3, s32[4,16,128]{2,1,0:T(8,128)} %bitcast.2, s32[4,128]{1,0:T(4,128)} %len_hbm.1, s32[4,128]{1,0:T(4,128)} %pick_hbm.1, ...), custom_call_target="tpu_custom_call" | custom-call | tf_op jit(solution)/shard_map/phantom/pallas_call | solution.py:348
  38.4 0.7 %copy.11 = bf16[4,128,128]{2,1,0:T(8,128)(2,1)} copy(bf16[4,128,128]{2,1,0:T(8,128)(2,1)S(1)} %get-tuple-element.2) | data formatting | bytes 262144
  39.1 0.6 %copy.12 = bf16[4,128]{1,0:T(4,128)(2,1)} copy(bf16[4,128]{1,0:T(4,128)(2,1)S(1)} %get-tuple-element.3) | data formatting | bytes 2048

commit v3 on v2

--- a/solution.py
+++ b/solution.py
@@ -51,7 +51,7 @@
     halo_v, unm_v, own_v, cand_v, len_v, pick_v, desc_v, right_v,
     send_v, recv_v, meta_s, meta_r, reply_v, back_v, bmeta_s, bmeta_r, bests,
     put_v, take_v, merit_v, picked_v, fields_v, res_v, found_v, shut_v,
-    load_sem, desc_sem, dsend, drecv, rsend, rrecv, msend, mrecv, psend, precv, bsend, brecv, xsend, xrecv, pair_sem,
+    load_sem, desc_sem, dsend, drecv, rsend, rrecv, msend, mrecv, psend, precv, bsend, brecv, xsend, xrecv, pair_sem, hsend, hrecv,
 ):
     me = lax.axis_index("space")
     core = lax.axis_index("rep")
@@ -61,7 +61,7 @@
     loads = [
         pltpu.make_async_copy(own_hbm, own_v, load_sem.at[0]),
         pltpu.make_async_copy(halo_hbm, halo_v, load_sem.at[1]),
-        pltpu.make_async_copy(cand_hbm.at[pl.ds(2 * core, 2)], cand_v, load_sem.at[2]),
+        pltpu.make_async_copy(cand_hbm, cand_v, load_sem.at[2]),
         pltpu.make_async_copy(unm_hbm, unm_v, load_sem.at[3]),
         pltpu.make_async_copy(len_hbm, len_v, load_sem.at[4]),
         pltpu.make_async_copy(pick_hbm, pick_v, load_sem.at[5]),
@@ -112,20 +112,19 @@
     spans, picks, lives = len_v[...], pick_v[...], unm_v[...]
     folded = jnp.zeros((PEERS, HALF), F32)
     place = iota((K, HALOS), 0)
-    for j in range(2):
-        def mine(a):
-            return jnp.where(first, a[j : j + 1, :], a[2 + j : 3 + j, :])
-        span = jnp.where(mine(lives) == 1, mine(spans), 0)
-        pick = jnp.where(mine(lives) == 1, mine(picks), -1)
-        slot = own_rank[j] + 2.0 * j
-        listed = cand_v[j]
+    for snap in range(4):
+        row = slice(snap, snap + 1)
+        span = jnp.where(lives[row] == 1, spans[row], 0)
+        pick = picks[row]
+        listed = cand_v[snap]
         coded = (listed - jnp.where(listed < 256, 256, 255)).astype(F32)
         chosen = jnp.sum(jnp.where(place == pick, coded, 0.0), axis=0, keepdims=True)
+        coded = jnp.where(place == 0, chosen, jnp.where(place == pick, coded[0:1, :], coded))
         coded = jnp.where(place < span, coded, 0.0)
-        tail = jnp.where(place == 0, chosen, 0.0)
-        field = jnp.concatenate([coded, tail] * SLOTS, axis=0)
-        field = jnp.where((sub_h // 32).astype(F32) == slot, field, 0.0)
-        folded = folded + mm_nt(own_hot[j], field.astype(BF16))
+        field = jnp.concatenate([coded] * (2 * SLOTS), axis=0)
+        slot = ranks[snap] + 2.0 * snap
+        field = jnp.where((sub_h // K).astype(F32) == slot, field, 0.0)
+        folded = folded + mm_nt(hots[snap].astype(BF16), field.astype(BF16))
     meta_s[...] = folded.reshape(PEERS, 1, HALF)
 
     pl.semaphore_wait(barrier, PEERS)
@@ -140,22 +139,28 @@
     def reach(step):
         return 4 + (1 - 2 * (step % 2)) * ((step + 1) // 2)
 
+    def mine_plane(turn):
+        even = 4 + (1 - 2 * (turn % 2)) * (2 * ((turn + 1) // 2))
+        odd = 4 - (1 - 2 * (turn % 2)) * (1 + 2 * (turn // 2))
+        return even * other + odd * core
+
     def remote(src, dst, send_sem, recv_sem, goal):
         pltpu.make_async_remote_copy(
             src_ref=src, dst_ref=dst, send_sem=send_sem, recv_sem=recv_sem,
             device_id=goal, device_id_type=MESH,
         ).start()
 
-    def send_lists(step, carry):
-        plane = ((mz + reach(step)) % 8) * 16
+    def send_lists(turn, carry):
+        dz = mine_plane(turn)
+        plane = ((mz + dz) % 8) * 16
         for spot in range(15):
             goal = plane + in_plane[spot]
-            remote(meta_s.at[goal], meta_r.at[me], msend, mrecv.at[step], (goal, core))
-
-        @pl.when(step < 7)
+            remote(meta_s.at[goal], meta_r.at[me], msend, mrecv.at[dz], (goal, core))
+
+        @pl.when(dz > 0)
         def _():
             goal = plane + in_plane[15]
-            remote(meta_s.at[goal], meta_r.at[me], msend, mrecv.at[step], (goal, core))
+            remote(meta_s.at[goal], meta_r.at[me], msend, mrecv.at[dz], (goal, core))
 
         return carry
 
@@ -163,25 +168,27 @@
         plane = ((mz + reach(step)) % 8) * 16
         for spot in range(15):
             goal = plane + in_plane[spot]
-            remote(send_v.at[core * PEERS + goal], recv_v.at[core * PEERS + me], rsend, rrecv.at[step], (goal, core))
+            remote(send_v.at[core * PEERS + goal], recv_v.at[core * PEERS + me], rsend, rrecv.at[reach(step)], (goal, core))
 
         @pl.when(step < 7)
         def _():
             goal = plane + in_plane[15]
-            remote(send_v.at[core * PEERS + goal], recv_v.at[core * PEERS + me], rsend, rrecv.at[step], (goal, core))
+            remote(send_v.at[core * PEERS + goal], recv_v.at[core * PEERS + me], rsend, rrecv.at[reach(step)], (goal, core))
 
         for spot in range(16):
             goal = plane + in_plane[spot]
-            remote(send_v.at[other * PEERS + goal], recv_v.at[core * PEERS + me], rsend, rrecv.at[step], (goal, other))
+            remote(send_v.at[other * PEERS + goal], recv_v.at[core * PEERS + me], rsend, rrecv.at[reach(step)], (goal, other))
         return carry
 
-    lax.fori_loop(0, 8, send_lists, 0)
+    lax.fori_loop(0, 4, send_lists, 0)
     pl.semaphore_wait(pair_sem, 1)
     lax.fori_loop(0, 8, send_requests, 0)
-    self_row = pltpu.make_async_copy(send_v.at[core * PEERS + me], recv_v.at[core * PEERS + me], rrecv.at[7])
-    self_meta = pltpu.make_async_copy(meta_s.at[me], meta_r.at[me], mrecv.at[7])
+    self_row = pltpu.make_async_copy(send_v.at[core * PEERS + me], recv_v.at[core * PEERS + me], rrecv.at[0])
     self_row.start()
-    self_meta.start()
+
+    @pl.when(core == 0)
+    def _():
+        pltpu.make_async_copy(meta_s.at[me], meta_r.at[me], mrecv.at[0]).start()
 
     col_id = iota((2 * HALOS, REQS), 1).astype(F32)
     live_cols = []
@@ -209,15 +216,32 @@
     even16 = (1.0 - odd).astype(BF16)
     lane_p = iota((16, HALF), 1)
 
+    def hand_on(turn, carry):
+        dz = mine_plane(3 - turn)
+        back = ((mz + 8 - dz) % 8) * 16
+        lists = meta_r.at[pl.ds(back, 16)]
+        pltpu.make_async_copy(lists, lists, mrecv.at[dz]).wait()
+        remote(lists, lists, hsend, hrecv.at[dz], (me, other))
+        return carry
+
+    lax.fori_loop(0, 4, hand_on, 0)
+
     def list_plane(turn, carry):
         step = 7 - turn
         back = ((mz + 8 - reach(step)) % 8) * 16
         base = pl.multiple_of(back * SLOTS, PLANE)
         at = pl.ds(base, PLANE)
-        pltpu.make_async_copy(meta_r.at[pl.ds(0, 16)], meta_r.at[pl.ds(0, 16)], mrecv.at[step]).wait()
+        theirs = (reach(step) + core) % 2 == 1
+
+        @pl.when(theirs)
+        def _():
+            pltpu.make_async_copy(meta_r.at[pl.ds(0, 16)], meta_r.at[pl.ds(0, 16)], hrecv.at[reach(step)]).wait()
+
         got = meta_r[pl.ds(back, 16)].reshape(16, HALF)
         for slot in range(SLOTS):
-            moved = got if slot == 0 else pltpu.roll(got, HALF - 32 * slot, 1)
+            shift = (HALF - K * slot) % HALF
+            here = pltpu.roll(got, shift, 1) if slot else got
+            moved = jnp.where(first, here, pltpu.roll(got, HALF // 2 - K * slot, 1))
             fields_v[pl.ds(base + slot, 16, stride=SLOTS), :] = moved
         for block in range(PLANE // ROWS):
             there = pl.ds(pl.multiple_of(base + block * ROWS, ROWS), ROWS)
@@ -226,7 +250,7 @@
             for k in range(K):
                 shut = jnp.where(field[:, k : k + 1] == code, 0.0, shut)
             shut_v[there, :] = shut
-            pick = field[:, K : K + 1] == code
+            pick = field[:, 0:1] == code
             picked_v[there, :] = jnp.where(pick, 1.0, 0.0).astype(BF16)
         picked = picked_v[at, :]
         for part in range(2):
@@ -241,7 +265,7 @@
         back = ((mz + 8 - reach(step)) % 8) * 16
         base = pl.multiple_of(back * SLOTS, PLANE)
         at = pl.ds(base, PLANE)
-        pltpu.make_async_copy(recv_v.at[pl.ds(0, 32)], recv_v.at[pl.ds(0, 32)], rrecv.at[step]).wait()
+        pltpu.make_async_copy(recv_v.at[pl.ds(0, 32)], recv_v.at[pl.ds(0, 32)], rrecv.at[reach(step)]).wait()
         rows = [recv_v[pl.ds(part * PEERS + back, 16)].reshape(PLANE, HALF) for part in range(2)]
         left = jnp.concatenate(
             [rows[0] * even16, rows[1] * even16, rows[0] * odd16, rows[1] * odd16], axis=1
@@ -281,7 +305,7 @@
     def reply_plane(step, carry):
         back = ((mz + 8 - reach(step)) % 8) * 16
         at = pl.ds(pl.multiple_of(back * SLOTS, PLANE), PLANE)
-        pick = fields_v[at, :][:, K : K + 1] == code
+        pick = fields_v[at, :][:, 0:1] == code
         claim = jnp.max(jnp.where(pick, col, NEG), axis=1, keepdims=True)
         quality = 1.0 + softplus(jnp.where(iota((PLANE, HALF), 1) < 64, claim, res_v[at, :]))
         claim_q, mine_q = quality[:, 0:1], quality[:, 64:65]
@@ -326,7 +350,16 @@
     )
     best_send.start()
     drain(send_v, rsend)
-    drain(meta_s, msend)
+
+    @pl.when(core == 0)
+    def _():
+        pltpu.make_async_copy(meta_s.at[pl.ds(0, 63)], meta_s.at[pl.ds(0, 63)], msend).wait()
+
+    @pl.when(core == 1)
+    def _():
+        pltpu.make_async_copy(meta_s.at[pl.ds(0, 64)], meta_s.at[pl.ds(0, 64)], msend).wait()
+
+    pltpu.make_async_copy(meta_s.at[pl.ds(0, 64)], meta_s.at[pl.ds(0, 64)], hsend).wait()
     drain(bmeta_s, bsend)
     best_send.wait()
     best_ref[...] = jnp.concatenate([bests[0, 0:2], bests[1, 0:2]], axis=0).astype(BF16)
@@ -341,11 +374,22 @@
     drain(reply_v, psend)
 
 
+def write_out(out_v, best_v, out_hbm, best_hbm, sems):
+    writes = [
+        pltpu.make_async_copy(out_v, out_hbm, sems.at[0]),
+        pltpu.make_async_copy(best_v, best_hbm, sems.at[1]),
+    ]
+    for write in writes:
+        write.start()
+    for write in writes:
+        write.wait()
+
+
 def body(halo_rows, unmatched, owner_id, cand_index, lengths, choice_index, desc_rows):
     any_space = pl.BlockSpec(memory_space=pl.ANY)
     vmem = pl.BlockSpec(memory_space=pltpu.VMEM)
     dma = pltpu.SemaphoreType.DMA
-    return pl.pallas_call(
+    out, best = pl.pallas_call(
         kernel,
         name="phantom",
         out_shape=(
@@ -358,7 +402,7 @@
             pltpu.VMEM((4, HALOS, HALF), BF16),
             pltpu.VMEM((4, HALOS), jnp.int32),
             pltpu.VMEM((4, HALOS), jnp.int32),
-            pltpu.VMEM((2, K, HALOS), jnp.int32),
+            pltpu.VMEM((4, K, HALOS), jnp.int32),
             pltpu.VMEM((4, HALOS), jnp.int32),
             pltpu.VMEM((4, HALOS), jnp.int32),
             pltpu.VMEM((2, 2, CANDS, HALF), BF16),
@@ -382,9 +426,21 @@
             pltpu.VMEM((REQS, CANDS), F32),
             dma((6,)), dma, dma, dma, dma, dma((8,)), dma, dma((8,)), dma, dma, dma, dma, dma, dma,
             pltpu.SemaphoreType.REGULAR,
+            dma, dma((8,)),
         ],
         compiler_params=pltpu.CompilerParams(collective_id=0, has_side_effects=True),
     )(halo_rows, unmatched, owner_id[:, :, 0], jnp.swapaxes(cand_index, 1, 2), lengths, choice_index, desc_rows)
+    return pl.pallas_call(
+        write_out,
+        name="write",
+        out_shape=(
+            jax.ShapeDtypeStruct(halo_rows.shape, BF16),
+            jax.ShapeDtypeStruct(unmatched.shape, BF16),
+        ),
+        in_specs=[vmem, vmem],
+        out_specs=(any_space, any_space),
+        scratch_shapes=[dma((2,))],
+    )(pltpu.with_memory_space_constraint(out, pltpu.VMEM), pltpu.with_memory_space_constraint(best, pltpu.VMEM))
 
 
 def solution(mesh):

time: 39.7 us -> 39.1 us (0.985)
  local copies, waits for them, and re-layouts: 1.22 us -> 0 us
  Pallas kernels: 37.8 us -> 38.4 us
    unnamed x2 -> x0, local copies, waits for them, and re-layouts: 1.22 us -> none
    pallas_call x0 -> x1, Pallas kernels: none -> 0.68 us  [body(): pl.pallas_call(write_out, name='write', out_shape=(jax.ShapeDtypeStruct(h...]
where the time goes in v3:
time: 39.1 us; the launch traced here: 39 us
  Pallas kernels  38.4 us (98%)
  between operations  0.64 us (2%)
    pallas_call x1, Pallas kernels, body(): pl.pallas_call(kernel, name='phantom', out_shape=(pltpu.VMEM(halo_rows.sh...  37.7 us

profile of v3, /device:TPU:1, one launch (start us, length us, event | category | flops | bytes accessed | tf_op | source)
XLA Modules:
  0.0 39.0 jit_solution(17526392907151507597)
XLA Ops:
  0.6 37.7 %phantom.1 = (bf16[4,128,128]{2,1,0:T(8,128)(2,1)S(1)}, bf16[4,128]{1,0:T(4,128)(2,1)S(1)}) custom-call(bf16[4,128,128]{2,1,0:T(8,128)(2,1)} %halo_hbm.1, s32[4,128]{1,0:T(4,128)} %unm_hbm.1, s32[4,128]{1,0:T(4,128)} %bitcast.3, s32[4,16,128]{2,1,0:T(8,128)} %bitcast.2, s32[4,128]{1,0:T(4,128)} %len_hbm.1, s32[4,128]{1,0:T(4,128)} %pick_hbm.1, ...), custom_call_target="tpu_custom_call" | custom-call | tf_op jit(solution)/shard_map/phantom/pallas_call | solution.py:392
  38.4 0.7 %write.1 = (bf16[4,128,128]{2,1,0:T(8,128)(2,1)}, bf16[4,128]{1,0:T(4,128)(2,1)}) custom-call(bf16[4,128,128]{2,1,0:T(8,128)(2,1)S(1)} %get-tuple-element.4.out_v, bf16[4,128]{1,0:T(4,128)(2,1)S(1)} %get-tuple-element.5.best_v), custom_call_target="tpu_custom_call" | custom-call | tf_op jit(solution)/shard_map/write/pallas_call | solution.py:433

commit v4 on v3

--- a/solution.py
+++ b/solution.py
@@ -49,9 +49,9 @@
     halo_hbm, unm_hbm, own_hbm, cand_hbm, len_hbm, pick_hbm, desc_hbm,
     out_ref, best_ref,
     halo_v, unm_v, own_v, cand_v, len_v, pick_v, desc_v, right_v,
-    send_v, recv_v, meta_s, meta_r, reply_v, back_v, bmeta_s, bmeta_r, bests,
-    put_v, take_v, merit_v, picked_v, fields_v, res_v, found_v, shut_v,
-    load_sem, desc_sem, dsend, drecv, rsend, rrecv, msend, mrecv, psend, precv, bsend, brecv, xsend, xrecv, pair_sem, hsend, hrecv,
+    send_v, recv_v, meta_s, meta_r, reply_v, back_v, bmeta_s, bmeta_r,
+    put_v, take_v, merit_v, picked_v, fields_v, res_v, found_v, shut_v, came_v,
+    load_sem, desc_sem, dsend, drecv, rsend, rrecv, msend, mrecv, psend, precv, bsend, brecv, pair_sem, hsend, hrecv,
 ):
     me = lax.axis_index("space")
     core = lax.axis_index("rep")
@@ -256,10 +256,26 @@
         for part in range(2):
             even_rows = mm(picked, desc_v[part, 0])
             odd_rows = mm(picked, desc_v[part, 1])
-            found_v[at, part * HALF : (part + 1) * HALF] = jnp.where(odd == 0.0, even_rows, odd_rows)
+            found = jnp.where(odd == 0.0, even_rows, odd_rows)
+            found_v[at, part * HALF : (part + 1) * HALF] = found
+            reply_v[pl.ds(part * PEERS + back, 16)] = found.astype(BF16).reshape(16, SLOTS, HALF)
+        for spot in range(16):
+            goal = back + in_plane[spot]
+            remote(reply_v.at[other * PEERS + goal], back_v.at[core * PEERS + me], psend, precv, (goal, other))
+        for spot in range(15):
+            goal = back + in_plane[spot]
+            remote(reply_v.at[core * PEERS + goal], back_v.at[core * PEERS + me], psend, precv, (goal, core))
+
+        @pl.when(step < 7)
+        def _():
+            goal = back + in_plane[15]
+            remote(reply_v.at[core * PEERS + goal], back_v.at[core * PEERS + me], psend, precv, (goal, core))
+
         return carry
 
     lax.fori_loop(0, 8, list_plane, 0)
+    self_back = pltpu.make_async_copy(reply_v.at[core * PEERS + me], back_v.at[core * PEERS + me], load_sem.at[0])
+    self_back.start()
 
     def score_plane(step, col):
         back = ((mz + 8 - reach(step)) % 8) * 16
@@ -280,19 +296,6 @@
             top = jnp.max(kept, axis=1, keepdims=True)
             res_v[there, :] = jnp.where(lane_r < 64, top, own_merit[block * ROWS : (block + 1) * ROWS]) * 0.0625
             col = jnp.maximum(col, jnp.max(kept.reshape(ROWS // 8, 8, CANDS), axis=0))
-        tops = jnp.zeros((16, HALF), F32)
-        for slot in range(SLOTS):
-            tops = jnp.where(lane_p == slot, res_v[pl.ds(base + slot, 16, stride=SLOTS), :], tops)
-        bmeta_s[pl.ds(back, 16)] = tops.reshape(16, 1, HALF)
-        for spot in range(15):
-            goal = back + in_plane[spot]
-            remote(bmeta_s.at[goal], bmeta_r.at[me], bsend, brecv, (goal, core))
-
-        @pl.when(step < 7)
-        def _():
-            goal = back + in_plane[15]
-            remote(bmeta_s.at[goal], bmeta_r.at[me], bsend, brecv, (goal, core))
-
         return col
 
     col = lax.fori_loop(0, 8, score_plane, jnp.full((8, CANDS), NEG, F32)) * 0.0625
@@ -304,51 +307,66 @@
 
     def reply_plane(step, carry):
         back = ((mz + 8 - reach(step)) % 8) * 16
-        at = pl.ds(pl.multiple_of(back * SLOTS, PLANE), PLANE)
+        base = pl.multiple_of(back * SLOTS, PLANE)
+        at = pl.ds(base, PLANE)
+        top = res_v[at, :][:, 0:1]
         pick = fields_v[at, :][:, 0:1] == code
         claim = jnp.max(jnp.where(pick, col, NEG), axis=1, keepdims=True)
         quality = 1.0 + softplus(jnp.where(iota((PLANE, HALF), 1) < 64, claim, res_v[at, :]))
         claim_q, mine_q = quality[:, 0:1], quality[:, 64:65]
         share = mine_q / (mine_q + claim_q)
-        for part in range(2):
-            blocks = pl.ds(part * PEERS + back, 16)
-            row = recv_v[blocks].reshape(PLANE, HALF).astype(F32)
-            blend = (1.0 - share) * row + share * found_v[at, part * HALF : (part + 1) * HALF]
-            reply_v[blocks] = blend.astype(BF16).reshape(16, SLOTS, HALF)
-        for spot in range(16):
+        res_v[at, :] = jnp.where(iota((PLANE, HALF), 1) < 64, share, top)
+        tops = jnp.zeros((16, HALF), F32)
+        for slot in range(SLOTS):
+            tops = jnp.where(lane_p % 64 == slot, res_v[pl.ds(base + slot, 16, stride=SLOTS), :], tops)
+        bmeta_s[pl.ds(back, 16)] = tops.reshape(16, 1, HALF)
+        def news_to(spot, to):
             goal = back + in_plane[spot]
-            remote(reply_v.at[other * PEERS + goal], back_v.at[core * PEERS + me], psend, precv, (goal, other))
+            remote(bmeta_s.at[goal], bmeta_r.at[core * PEERS + me], bsend, brecv, (goal, to))
+
         for spot in range(15):
-            goal = back + in_plane[spot]
-            remote(reply_v.at[core * PEERS + goal], back_v.at[core * PEERS + me], psend, precv, (goal, core))
+            news_to(spot, core)
+            news_to(spot, other)
 
         @pl.when(step < 7)
         def _():
-            goal = back + in_plane[15]
-            remote(reply_v.at[core * PEERS + goal], back_v.at[core * PEERS + me], psend, precv, (goal, core))
-
+            news_to(15, core)
+
+        news_to(15, other)
         return carry
 
     lax.fori_loop(0, 8, reply_plane, 0)
-    self_back = pltpu.make_async_copy(reply_v.at[core * PEERS + me], back_v.at[core * PEERS + me], load_sem.at[0])
-    self_best = pltpu.make_async_copy(bmeta_s.at[me], bmeta_r.at[me], load_sem.at[1])
-    self_back.start()
+    self_best = pltpu.make_async_copy(bmeta_s.at[me], bmeta_r.at[core * PEERS + me], load_sem.at[1])
     self_best.start()
+    self_back.wait()
+    drain(back_v, precv)
+    for pair in range(2):
+        came_v[pair] = mm(take_v[pair], back_v[pair * PEERS : (pair + 1) * PEERS].reshape(REQS, HALF))
+
     self_best.wait()
     drain(bmeta_r, brecv)
-    tops_back = bmeta_r[...].reshape(PEERS, HALF).astype(BF16)
     best_rows = []
-    for j in range(2):
-        found = mm_tn(tops_back, own_hot[j])
-        value = jnp.where(own_rank[j] == 0.0, found[2 * j : 2 * j + 1, :], found[2 * j + 1 : 2 * j + 2, :])
-        live = jnp.where(first, lives[j : j + 1, :], lives[2 + j : 3 + j, :])
-        best_rows.append(jnp.where(live == 1, value, 0.0))
-    bests[core] = jnp.concatenate(best_rows + [jnp.zeros((6, HALOS), F32)], axis=0)
-    best_send = pltpu.make_async_remote_copy(
-        src_ref=bests.at[core], dst_ref=bests.at[core],
-        send_sem=xsend, recv_sem=xrecv, device_id=(me, other), device_id_type=MESH,
-    )
-    best_send.start()
+    for pair in range(2):
+        news = bmeta_r[pair * PEERS : (pair + 1) * PEERS].reshape(PEERS, HALF)
+        news_hi = news.astype(BF16)
+        news_lo = (news - news_hi.astype(F32)).astype(BF16)
+        share_rows = []
+        for j in range(2):
+            snap = 2 * pair + j
+            hot = hots[snap].astype(BF16)
+            coarse = mm_tn(news_hi, hot)
+            fine = coarse + mm_tn(news_lo, hot)
+            zero = ranks[snap] == 0.0
+            best = jnp.where(zero, coarse[64 + 2 * j : 65 + 2 * j, :], coarse[65 + 2 * j : 66 + 2 * j, :])
+            best_rows.append(jnp.where(lives[snap : snap + 1, :] == 1, best, 0.0))
+            share_rows.append(jnp.where(zero, fine[2 * j : 2 * j + 1, :], fine[2 * j + 1 : 2 * j + 2, :]))
+        cols = jnp.concatenate(share_rows + [jnp.zeros((HALOS - 2, HALOS), F32)], axis=0).T
+        share = jnp.concatenate([cols[:, 0:1], cols[:, 1:2]], axis=0)
+        kept = halo_v[2 * pair : 2 * pair + 2].reshape(2 * HALOS, HALF).astype(F32)
+        blend = (1.0 - share) * kept + share * came_v[pair]
+        out = jnp.where(put_v[pair] == 1.0, blend, kept)
+        out_ref[2 * pair : 2 * pair + 2] = out.astype(BF16).reshape(2, HALOS, HALF)
+    best_ref[...] = jnp.concatenate(best_rows, axis=0).astype(BF16)
     drain(send_v, rsend)
 
     @pl.when(core == 0)
@@ -360,17 +378,7 @@
         pltpu.make_async_copy(meta_s.at[pl.ds(0, 64)], meta_s.at[pl.ds(0, 64)], msend).wait()
 
     pltpu.make_async_copy(meta_s.at[pl.ds(0, 64)], meta_s.at[pl.ds(0, 64)], hsend).wait()
-    drain(bmeta_s, bsend)
-    best_send.wait()
-    best_ref[...] = jnp.concatenate([bests[0, 0:2], bests[1, 0:2]], axis=0).astype(BF16)
-
-    self_back.wait()
-    drain(back_v, precv)
-    for pair in range(2):
-        came = mm(take_v[pair], back_v[pair * PEERS : (pair + 1) * PEERS].reshape(REQS, HALF))
-        kept = halo_v[2 * pair : 2 * pair + 2].reshape(2 * HALOS, HALF).astype(F32)
-        out = jnp.where(put_v[pair] == 1.0, came, kept)
-        out_ref[2 * pair : 2 * pair + 2] = out.astype(BF16).reshape(2, HALOS, HALF)
+    drain(bmeta_r, bsend)
     drain(reply_v, psend)
 
 
@@ -414,8 +422,7 @@
             pltpu.VMEM((2 * PEERS, SLOTS, HALF), BF16),
             pltpu.VMEM((2 * PEERS, SLOTS, HALF), BF16),
             pltpu.VMEM((PEERS, 1, HALF), F32),
-            pltpu.VMEM((PEERS, 1, HALF), F32),
-            pltpu.VMEM((2, 8, HALOS), F32),
+            pltpu.VMEM((2 * PEERS, 1, HALF), F32),
             pltpu.VMEM((2, 2 * HALOS, HALF), F32),
             pltpu.VMEM((2, 2 * HALOS, REQS), BF16),
             pltpu.VMEM((PLANE, CANDS), F32),
@@ -424,7 +431,8 @@
             pltpu.VMEM((REQS, HALF), F32),
             pltpu.VMEM((REQS, 2 * HALF), F32),
             pltpu.VMEM((REQS, CANDS), F32),
-            dma((6,)), dma, dma, dma, dma, dma((8,)), dma, dma((8,)), dma, dma, dma, dma, dma, dma,
+            pltpu.VMEM((2, 2 * HALOS, HALF), F32),
+            dma((6,)), dma, dma, dma, dma, dma((8,)), dma, dma((8,)), dma, dma, dma, dma,
             pltpu.SemaphoreType.REGULAR,
             dma, dma((8,)),
         ],

time: 39.1 us -> 38.2 us (0.977)
  Pallas kernels: 38.4 us -> 37.5 us
    pallas_call x1, Pallas kernels: 37.7 us -> 36.8 us  [body(): pl.pallas_call(kernel, name='phantom', out_shape=(pltpu.VMEM(halo_rows.sh...]
where the time goes in v4:
time: 38.2 us; the launch traced here: 38.1 us
  Pallas kernels  37.5 us (98%)
  between operations  0.64 us (2%)
    pallas_call x1, Pallas kernels, body(): pl.pallas_call(kernel, name='phantom', out_shape=(pltpu.VMEM(halo_rows.sh...  36.8 us

profile of v4, /device:TPU:1, one launch (start us, length us, event | category | flops | bytes accessed | tf_op | source)
XLA Modules:
  0.0 38.1 jit_solution(11291922531812572528)
XLA Ops:
  0.6 36.8 %phantom.1 = (bf16[4,128,128]{2,1,0:T(8,128)(2,1)S(1)}, bf16[4,128]{1,0:T(4,128)(2,1)S(1)}) custom-call(bf16[4,128,128]{2,1,0:T(8,128)(2,1)} %halo_hbm.1, s32[4,128]{1,0:T(4,128)} %unm_hbm.1, s32[4,128]{1,0:T(4,128)} %bitcast.3, s32[4,16,128]{2,1,0:T(8,128)} %bitcast.2, s32[4,128]{1,0:T(4,128)} %len_hbm.1, s32[4,128]{1,0:T(4,128)} %pick_hbm.1, ...), custom_call_target="tpu_custom_call" | custom-call | tf_op jit(solution)/shard_map/phantom/pallas_call | solution.py:400
  37.5 0.7 %write.1 = (bf16[4,128,128]{2,1,0:T(8,128)(2,1)}, bf16[4,128]{1,0:T(4,128)(2,1)}) custom-call(bf16[4,128,128]{2,1,0:T(8,128)(2,1)S(1)} %get-tuple-element.4.out_v, bf16[4,128]{1,0:T(4,128)(2,1)S(1)} %get-tuple-element.5.best_v), custom_call_target="tpu_custom_call" | custom-call | tf_op jit(solution)/shard_map/write/pallas_call | solution.py:441

commit v5 on v4

--- a/solution.py
+++ b/solution.py
@@ -166,18 +166,20 @@
 
     def send_requests(step, carry):
         plane = ((mz + reach(step)) % 8) * 16
+
+        def to_core(spot, to):
+            goal = plane + in_plane[spot]
+            remote(send_v.at[to * PEERS + goal], recv_v.at[core * PEERS + me], rsend, rrecv.at[reach(step)], (goal, to))
+
         for spot in range(15):
-            goal = plane + in_plane[spot]
-            remote(send_v.at[core * PEERS + goal], recv_v.at[core * PEERS + me], rsend, rrecv.at[reach(step)], (goal, core))
+            to_core(spot, core)
+            to_core(spot, other)
 
         @pl.when(step < 7)
         def _():
-            goal = plane + in_plane[15]
-            remote(send_v.at[core * PEERS + goal], recv_v.at[core * PEERS + me], rsend, rrecv.at[reach(step)], (goal, core))
-
-        for spot in range(16):
-            goal = plane + in_plane[spot]
-            remote(send_v.at[other * PEERS + goal], recv_v.at[core * PEERS + me], rsend, rrecv.at[reach(step)], (goal, other))
+            to_core(15, core)
+
+        to_core(15, other)
         return carry
 
     lax.fori_loop(0, 4, send_lists, 0)
@@ -259,18 +261,19 @@
             found = jnp.where(odd == 0.0, even_rows, odd_rows)
             found_v[at, part * HALF : (part + 1) * HALF] = found
             reply_v[pl.ds(part * PEERS + back, 16)] = found.astype(BF16).reshape(16, SLOTS, HALF)
-        for spot in range(16):
+        def row_to(spot, to):
             goal = back + in_plane[spot]
-            remote(reply_v.at[other * PEERS + goal], back_v.at[core * PEERS + me], psend, precv, (goal, other))
+            remote(reply_v.at[to * PEERS + goal], back_v.at[core * PEERS + me], psend, precv, (goal, to))
+
         for spot in range(15):
-            goal = back + in_plane[spot]
-            remote(reply_v.at[core * PEERS + goal], back_v.at[core * PEERS + me], psend, precv, (goal, core))
+            row_to(spot, core)
+            row_to(spot, other)
 
         @pl.when(step < 7)
         def _():
-            goal = back + in_plane[15]
-            remote(reply_v.at[core * PEERS + goal], back_v.at[core * PEERS + me], psend, precv, (goal, core))
-
+            row_to(15, core)
+
+        row_to(15, other)
         return carry
 
     lax.fori_loop(0, 8, list_plane, 0)

time: 38.2 us -> 38.2 us (level)
  no operation moved by 1% of the time
where the time goes in v5:
time: 38.2 us; the launch traced here: 38.1 us
  Pallas kernels  37.4 us (98%)
  between operations  0.64 us (2%)
    pallas_call x1, Pallas kernels, body(): pl.pallas_call(kernel, name='phantom', out_shape=(pltpu.VMEM(halo_rows.sh...  36.7 us

profile of v5, /device:TPU:1, one launch (start us, length us, event | category | flops | bytes accessed | tf_op | source)
XLA Modules:
  0.0 38.1 jit_solution(14983263152049207202)
XLA Ops:
  0.6 36.7 %phantom.1 = (bf16[4,128,128]{2,1,0:T(8,128)(2,1)S(1)}, bf16[4,128]{1,0:T(4,128)(2,1)S(1)}) custom-call(bf16[4,128,128]{2,1,0:T(8,128)(2,1)} %halo_hbm.1, s32[4,128]{1,0:T(4,128)} %unm_hbm.1, s32[4,128]{1,0:T(4,128)} %bitcast.3, s32[4,16,128]{2,1,0:T(8,128)} %bitcast.2, s32[4,128]{1,0:T(4,128)} %len_hbm.1, s32[4,128]{1,0:T(4,128)} %pick_hbm.1, ...), custom_call_target="tpu_custom_call" | custom-call | tf_op jit(solution)/shard_map/phantom/pallas_call | solution.py:403
  37.4 0.7 %write.1 = (bf16[4,128,128]{2,1,0:T(8,128)(2,1)}, bf16[4,128]{1,0:T(4,128)(2,1)}) custom-call(bf16[4,128,128]{2,1,0:T(8,128)(2,1)S(1)} %get-tuple-element.4.out_v, bf16[4,128]{1,0:T(4,128)(2,1)S(1)} %get-tuple-element.5.best_v), custom_call_target="tpu_custom_call" | custom-call | tf_op jit(solution)/shard_map/write/pallas_call | solution.py:444
